TPU v7x, 16 devices: a 4x2x1 block of a 4x4x8 slice. The times are simulated.
16 devices in a mesh: dp: 2 (over y, z), sp: 8 (over x, core).
Axes of the slice: x: 4, y: 2, z: 1, core: 2. Of those that a mesh axis runs over, the one named last changes fastest.
The devices are a block of a 4x4x8 slice.
Arguments:
- q: bfloat16 [64, 32, 64], P('dp'), parts along dimension 0
- k: bfloat16 [64, 4096, 32, 64], P('dp', 'sp'), parts along dimension 0
- v: bfloat16 [64, 4096, 32, 64], P('dp', 'sp'), parts along dimension 0
Outputs:
- q: bfloat16 [64, 32, 64], P('dp'), parts along dimension 0
There are 2 independent parts. A program takes and returns all parts, laid end to end along the dimension named above; each array names one.
All inputs are finite; a program needn't handle non-finite values.
Results may differ from a plain program's by a relative error of at most 0.012.
Values are sent between devices in bfloat16 or wider.
A program may use at most 768 MiB of HBM per device.

v0:
```python
import jax
import jax.numpy as jnp
from jax import lax
from jax.sharding import PartitionSpec as P


def einsum(form, a, b):
    return jnp.einsum(form, a.astype(jnp.float32), b.astype(jnp.float32))


def part_of(q, k, v):
    grouped = q.reshape(q.shape[0], k.shape[2], -1, q.shape[2])
    scores = einsum("bgsd,bugd->bgsu", grouped, k) * q.shape[2] ** -0.5
    high = jnp.max(scores, -1, keepdims=True)
    weights = jnp.exp(scores - high)
    seen = einsum("bgsu,bugd->bgsd", weights.astype(jnp.bfloat16), v)
    return jnp.concatenate([seen, jnp.sum(weights, -1, keepdims=True), high], -1)


def together(parts):
    seen, total, high = parts[..., :-2], parts[..., -2:-1], parts[..., -1:]
    scale = jnp.exp(high - jnp.max(high, 0))
    return (jnp.sum(seen * scale, 0) / jnp.sum(total * scale, 0)).astype(jnp.bfloat16)


def solution(mesh):
    def step(q, k, v):
        return together(lax.all_gather(part_of(q, k, v), "sp")).reshape(q.shape)

    return jax.shard_map(
        step,
        mesh=mesh,
        in_specs=(P("dp", None, None), P("dp", "sp", None, None), P("dp", "sp", None, None)),
        out_specs=P("dp", None, None),
        check_vma=False,
    )
```

profile of v0, /device:TPU:113, one launch (start us, length us, event | category | flops | bytes accessed | tf_op | source)
XLA Modules:
  0.0 111.2 jit_solution(10862572293812368850)
XLA Ops:
  6.5 0.0 all-gather.3.cloned.1.call-start
  6.6 22.7 %fusion.7 = f32[32,32,1,512]{3,2,1,0:T(1,128)S(1)} fusion(bf16[32,512,32,64]{1,3,2,0:T(8,128)(2,1)} %param.4, bf16[32,32,64,1]{2,1,0,3:T(8,128)(2,1)} %bitcast.26), kind=kOutput, calls=%fused_computation.12 | convolution fusion | flops 67108864 | bytes 69337088 | tf_op jit(solution)/shard_map/bgsd,bugd->bgsu/dot_general | solution.py:8
  29.3 0.2 fusion.5
  29.5 0.6 fusion.6
  30.1 0.3 copy.17
  30.4 0.3 copy.16
  30.6 25.6 %fusion.1 = f32[32,32,1,64]{3,2,1,0:T(1,128)S(1)} fusion(bf16[32,512,32,64]{1,3,2,0:T(8,128)(2,1)} %param.5, bf16[32,32,512,1]{2,1,0,3:T(8,128)(2,1)S(1)} %get-tuple-element.7), kind=kOutput, calls=%fused_computation.3 | convolution fusion | flops 67108864 | bytes 68419584 | tf_op jit(solution)/shard_map/bgsu,bugd->bgsd/dot_general | solution.py:8
  56.2 1.2 %pad_maximum_fusion = f32[32,32,1,66]{3,1,2,0:T(8,128)} fusion(f32[32,32,1,1]{3,1,2,0:T(8,128)S(1)} %copy.17, f32[32,32,1,1]{3,1,2,0:T(8,128)S(1)} %copy.16, f32[32,32,1,64]{3,1,2,0:T(8,128)S(1)} %bitcast.27), kind=kLoop, calls=%fused_computation.11 | loop fusion | flops 135168 | bytes 540672 | tf_op jit(solution)/shard_map/concatenate | solution.py:17
  57.4 0.1 all-gather.3.cloned.1.call-update
  57.5 31.2 %all-gather.3.cloned.1.call-done = f32[256,32,1,66]{3,1,2,0:T(8,128)} async-done(((f32[32,32,1,66]{3,1,2,0:T(8,128)}), f32[256,32,1,66]{3,1,2,0:T(8,128)}) %all-gather.3.cloned.1.call-update) | async-done | bytes 2162704 | tf_op jit(solution)/shard_map/all_gather | solution.py:28
  88.7 7.6 %copy.18 = f32[256,32,1,66]{1,0,3,2:T(8,128)} copy(f32[256,32,1,66]{3,1,2,0:T(8,128)} %all-gather.3.cloned.1.call-done) | data formatting | bytes 4325376 | tf_op jit(solution)/shard_map/all_gather | solution.py:28
  96.3 0.9 slice_reduce_fusion
  97.2 1.0 fusion.9
  98.2 4.7 %fusion = f32[32,32,64]{1,0,2:T(8,128)S(1)} fusion(f32[8,32,32,1,66]{2,1,0,4,3:T(8,128)} %bitcast.25, f32[8,32,32]{2,1,0:T(8,128)S(1)} %get-tuple-element.6), kind=kLoop, calls=%fused_computation.1 | loop fusion | flops 983040 | bytes 2392064 | tf_op jit(solution)/shard_map/reduce_sum | solution.py:23
  102.9 0.1 divide_convert_fusion
  103.0 1.3 %copy.19 = bf16[32,32,64]{2,1,0:T(8,128)(2,1)} copy(bf16[32,32,64]{1,0,2:T(8,128)(2,1)S(1)} %divide_convert_fusion) | data formatting | bytes 262144 | tf_op jit(solution)/shard_map/convert_element_type | solution.py:23
Async XLA Ops:
  6.5 82.1 %all-gather.3.cloned.1.call-start = ((), (), s32[]{:S(2)}) async-start(), calls=%async_computation | async-start | bytes 4718592 | tf_op jit(solution)/shard_map/all_gather | solution.py:28
Sparse Core Ops, SparseCore 0:
  57.6 31.0 all-gather.2
where the time goes:
time: 112 us; the launch traced here: 111 us
  matrix products  48.3 us (43%)
  waiting for transfers between devices  31.3 us (28%)
  between operations  13.5 us (12%)
  local copies, waits for them, and re-layouts  9.44 us (8%)
  other arithmetic  8.72 us (8%)
    dot_general x2, matrix products, einsum(): return jnp.einsum(form, a.astype(jnp.float32), b.astype(jnp.float32))  48.3 us
    all_gather x1, waiting for transfers between devices, step(): return together(lax.all_gather(part_of(q, k, v), 'sp')).reshape(q.shape)  31.2 us
    all_gather x1, local copies, waits for them, and re-layouts, step(): return together(lax.all_gather(part_of(q, k, v), 'sp')).reshape(q.shape)  7.62 us
    reduce_sum x1, other arithmetic, together(): jnp.sum(seen * scale, 0) / jnp.sum(total * scale, 0)  4.69 us
  transfers between devices with their start and end apart: 1, of which 1 were waited for; matrix products, arithmetic and copies ran while one was open for 0% of the time, Pallas kernels for 0%

commit v1 on v0

v1 whole, which is shorter than its diff:
```python
import functools

import jax
import jax.numpy as jnp
from jax import lax
from jax.experimental import pallas as pl
from jax.experimental.pallas import tpu as pltpu
from jax.sharding import PartitionSpec as P

ROWS = 8
SLOTS = 6
ENDS = (8, 16, 24, 28, 30, 31, 32)


def kernel(n, q_hbm, k_hbm, v_hbm, o_ref, qbuf, kbuf, vbuf, wbuf, parts, stats, q_sem, k_sem, v_sem, send_sem, recv_sem):
    batch, heads, dim = q_hbm.shape
    tokens = k_hbm.shape[2]
    chunks, wide = heads // ROWS, ROWS * dim
    me = lax.axis_index("sp")
    ends = tuple(e for e in ENDS if e < batch) + (batch,)
    f32 = jnp.float32

    def fetch(hbm, buf, sem, b):
        slot = lax.rem(b, SLOTS)
        return pltpu.make_async_copy(hbm.at[b], buf.at[slot], sem.at[slot])

    q_copy = pltpu.make_async_copy(q_hbm, qbuf, q_sem)
    q_copy.start()
    for b in range(SLOTS):
        fetch(k_hbm, kbuf, k_sem, b).start()
        fetch(v_hbm, vbuf, v_sem, b).start()

    barrier = pltpu.get_barrier_semaphore()
    for j in range(1, n):
        pl.semaphore_signal(barrier, inc=1, device_id={"sp": lax.rem(me + j, n)}, device_id_type=pl.DeviceIdType.MESH)

    row = lax.broadcasted_iota(jnp.int32, (ROWS, wide), 0)
    col = lax.broadcasted_iota(jnp.int32, (ROWS, wide), 1)
    own = (col // dim) == row
    lane = lax.broadcasted_iota(jnp.int32, (ROWS, 128), 1)
    even = (lax.broadcasted_iota(jnp.int32, (ROWS, 128), 0) % 2) == 0
    first = (lane < dim) == even

    def score(b, held):
        slot = lax.rem(b, SLOTS)
        highs, totals = held
        for c in range(chunks):
            query = qbuf[b, c * ROWS : (c + 1) * ROWS, :].astype(f32)
            spread = jnp.where(own, jnp.concatenate([query] * ROWS, axis=1), 0.0).astype(jnp.bfloat16)
            s = jnp.dot(spread, kbuf[slot, c * wide : (c + 1) * wide, :], preferred_element_type=f32) * dim**-0.5
            high = jnp.max(s, -1, keepdims=True)
            w = jnp.exp(s - high)
            total = jnp.sum(w, -1, keepdims=True)
            wbuf[c] = w.astype(jnp.bfloat16)
            here = lane == b * chunks + c
            highs = jnp.where(here, high, highs)
            totals = jnp.where(here, total, totals)
        return highs, totals

    def see(b):
        slot = lax.rem(b, SLOTS)
        seen = []
        for c in range(chunks):
            r = lax.dot_general(wbuf[c], vbuf[slot, c * wide : (c + 1) * wide, :], (((1,), (1,)), ((), ())), preferred_element_type=f32)
            r = jnp.where(own, r, 0.0)
            seen.append(sum(r[:, i * 128 : (i + 1) * 128] for i in range(wide // 128)))
        pairs = [seen[c] + pltpu.roll(seen[c + 1], dim, 1) for c in range(0, chunks, 2)]
        parts[me, b] = jnp.concatenate(pairs, 0).astype(jnp.bfloat16)

    def body(t, held):
        fetch(k_hbm, kbuf, k_sem, t).wait()
        fetch(v_hbm, vbuf, v_sem, t - 1).wait()
        see(t - 1)
        held = score(t, held)

        @pl.when(t + SLOTS < batch)
        def _():
            fetch(k_hbm, kbuf, k_sem, t + SLOTS).start()

        @pl.when(t - 1 + SLOTS < batch)
        def _():
            fetch(v_hbm, vbuf, v_sem, t - 1 + SLOTS).start()

        return held

    def copies(s, lo, hi, j, source):
        to = {"sp": lax.rem(me + j, n)}
        return [
            pltpu.make_async_remote_copy(
                src_ref=ref, dst_ref=ref, send_sem=send_sem.at[s, j - 1, x], recv_sem=recv_sem.at[s, j - 1, x],
                device_id=to, device_id_type=pl.DeviceIdType.MESH,
            )
            for x, ref in enumerate((parts.at[source, pl.ds(lo, hi - lo)], stats.at[source, s]))
        ]

    def send(s, lo, hi):
        for j in range(1, n):
            for copy in copies(s, lo, hi, j, me):
                copy.start()

    def together(s, lo, hi):
        for j in range(1, n):
            for copy in copies(s, lo, hi, j, lax.rem(me + n - j, n)):
                copy.wait_recv()
        high = stats[0, s, 0]
        for i in range(1, n):
            high = jnp.maximum(high, stats[i, s, 0])
        scales = [jnp.exp(stats[i, s, 0] - high) for i in range(n)]
        total = sum(stats[i, s, 1] * scales[i] for i in range(n))
        scales = [x / total for x in scales]
        for b in range(lo, hi):
            sums = [0.0] * (chunks // 2)
            for i in range(n):
                part = parts[i, b].astype(f32)
                for p in range(chunks // 2):
                    at = b * chunks + 2 * p
                    factor = jnp.where(first, scales[i][:, at : at + 1], scales[i][:, at + 1 : at + 2])
                    sums[p] += part[p * ROWS : (p + 1) * ROWS] * factor
            out = []
            for x in sums:
                y = pltpu.roll(x, dim, 1)
                out += [jnp.where(even, x, y)[:, :dim], jnp.where(even, y, x)[:, :dim]]
            o_ref[b] = jnp.concatenate(out, 0).astype(o_ref.dtype)

    q_copy.wait()
    fetch(k_hbm, kbuf, k_sem, 0).wait()
    zero = jnp.zeros((ROWS, 128), f32)
    held = score(0, (zero, zero))
    fetch(k_hbm, kbuf, k_sem, SLOTS).start()
    lo = 0
    done = []
    for s, hi in enumerate(ends):
        if hi < batch:
            held = lax.fori_loop(lo + 1, hi + 1, body, held)
        else:
            held = lax.fori_loop(lo + 1, hi, body, held)
            fetch(v_hbm, vbuf, v_sem, batch - 1).wait()
            see(batch - 1)
        stats[me, s, 0], stats[me, s, 1] = held
        if s == 0:
            pl.semaphore_wait(barrier, n - 1)
        send(s, lo, hi)
        done.append((s, lo, hi))
        if s >= 1 and s < len(ends) - 1:
            together(*done[s - 1])
        lo = hi
    for seg in done[-2:]:
        together(*seg)
    for s, lo, hi in done:
        for j in range(1, n):
            for copy in copies(s, lo, hi, j, me):
                copy.wait_send()


def solution(mesh):
    n = mesh.shape["sp"]

    def step(q, k, v):
        batch, tokens, heads, dim = k.shape
        k, v = (x.transpose(0, 2, 3, 1).reshape(batch, heads * dim, tokens) for x in (k, v))
        segments = len([e for e in ENDS if e < batch]) + 1
        hbm = pl.BlockSpec(memory_space=pltpu.HBM)
        return pl.pallas_call(
            functools.partial(kernel, n),
            out_shape=jax.ShapeDtypeStruct(q.shape, q.dtype),
            in_specs=[hbm] * 3,
            out_specs=pl.BlockSpec(memory_space=pltpu.VMEM),
            scratch_shapes=[
                pltpu.VMEM(q.shape, q.dtype),
                pltpu.VMEM((SLOTS, heads * dim, tokens), k.dtype),
                pltpu.VMEM((SLOTS, heads * dim, tokens), v.dtype),
                pltpu.VMEM((heads // ROWS, ROWS, tokens), jnp.bfloat16),
                pltpu.VMEM((n, batch, heads // 2, 2 * dim), jnp.bfloat16),
                pltpu.VMEM((n, segments, 2, ROWS, 128), jnp.float32),
                pltpu.SemaphoreType.DMA,
                pltpu.SemaphoreType.DMA((SLOTS,)),
                pltpu.SemaphoreType.DMA((SLOTS,)),
                pltpu.SemaphoreType.DMA((segments, n - 1, 2)),
                pltpu.SemaphoreType.DMA((segments, n - 1, 2)),
            ],
            compiler_params=pltpu.CompilerParams(collective_id=0, has_side_effects=True, vmem_limit_bytes=40 * 2**20),
            cost_estimate=pl.CostEstimate(flops=4 * k.size, bytes_accessed=4 * k.size, transcendentals=batch * heads * tokens),
        )(q, k, v)

    return jax.shard_map(
        step,
        mesh=mesh,
        in_specs=(P("dp", None, None), P("dp", "sp", None, None), P("dp", "sp", None, None)),
        out_specs=P("dp", None, None),
        check_vma=False,
    )
```

time: 112 us -> 56.3 us (0.50)
  Pallas kernels: 0 us -> 54.5 us
  matrix products: 48.3 us -> 0 us
  waiting for transfers between devices: 31.3 us -> 0 us
  between operations: 13.5 us -> 0.01 us
  other arithmetic: 8.72 us -> 0 us
  local copies, waits for them, and re-layouts: 9.44 us -> 1.65 us
    pallas_call x0 -> x1, Pallas kernels: none -> 54.5 us  [step(): pl.pallas_call(functools.partial(kernel, n), out_shape=jax.ShapeDtypeStru...]
    dot_general x2 -> x0, matrix products: 48.3 us -> none  [einsum(): return jnp.einsum(form, a.astype(jnp.float32), b.astype(jnp.float32))]
    all_gather x1 -> x0, waiting for transfers between devices: 31.2 us -> none  [step(): return together(lax.all_gather(part_of(q, k, v), 'sp')).reshape(q.shape)]
    all_gather x1 -> x0, local copies, waits for them, and re-layouts: 7.62 us -> none  [step(): return together(lax.all_gather(part_of(q, k, v), 'sp')).reshape(q.shape)]
    reduce_sum x2 -> x0, other arithmetic: 5.69 us -> none  [the longest x1 4.69 us: together(): jnp.sum(seen * scale, 0) / jnp.sum(total * scale, 0)]
    unnamed x0 -> x3, local copies, waits for them, and re-layouts: none -> 1.65 us
    convert_element_type x1 -> x0, local copies, waits for them, and re-layouts: 1.27 us -> none  [together(): (jnp.sum(seen * scale, 0) / jnp.sum(total * scale, 0)).astype(jnp.bfloat16)]
    concatenate x1 -> x0, other arithmetic: 1.18 us -> none  [part_of(): jnp.concatenate([seen, jnp.sum(weights, -1, keepdims=True), high], -1)]
  transfers between devices with their start and end apart: 1 -> 0, of which waited for: 1 -> 0; matrix products, arithmetic and copies ran while one was open for 0% -> 0% of each run, Pallas kernels for 0% -> 0%
where the time goes in v1:
time: 56.3 us; the launch traced here: 56.2 us
  Pallas kernels  54.5 us (97%)
  local copies, waits for them, and re-layouts  1.65 us (3%)
    pallas_call x1, Pallas kernels, step(): pl.pallas_call(functools.partial(kernel, n), out_shape=jax.ShapeDtypeStru...  54.5 us
    unnamed x3, local copies, waits for them, and re-layouts  1.65 us

profile of v1, /device:TPU:113, one launch (start us, length us, event | category | flops | bytes accessed | tf_op | source)
XLA Modules:
  0.0 56.2 jit_solution(10666456686850234021)
XLA Ops:
  0.0 0.0 copy-start
  0.0 0.9 %copy-done = bf16[32,32,64]{2,1,0:T(8,128)(2,1)S(1)} copy-done((bf16[32,32,64]{2,1,0:T(8,128)(2,1)S(1)}, bf16[32,32,64]{2,1,0:T(8,128)(2,1)}, u32[]{:S(2)}) %copy-start) | copy-done | bytes 131096
  1.0 54.5 %shard_map.37 = bf16[32,32,64]{2,1,0:T(8,128)(2,1)S(1)} custom-call(bf16[32,32,64]{2,1,0:T(8,128)(2,1)S(1)} %copy-done, bf16[32,2048,512]{2,1,0:T(8,128)(2,1)} %bitcast.1.k_hbm, bf16[32,2048,512]{2,1,0:T(8,128)(2,1)} %bitcast.3.v_hbm), custom_call_target="tpu_custom_call" | custom-call | flops 134217728 | bytes 134217728 | tf_op jit(solution)/shard_map/pallas_call | solution.py:163
  55.5 0.7 %copy.5 = bf16[32,32,64]{2,1,0:T(8,128)(2,1)} copy(bf16[32,32,64]{2,1,0:T(8,128)(2,1)S(1)} %shard_map.37) | data formatting | bytes 262144
Async XLA Ops:
  0.0 0.9 %copy-start = (bf16[32,32,64]{2,1,0:T(8,128)(2,1)S(1)}, bf16[32,32,64]{2,1,0:T(8,128)(2,1)}, u32[]{:S(2)}) copy-start(bf16[32,32,64]{2,1,0:T(8,128)(2,1)} %q_hbm.1) | copy-start | bytes 393220

commit v2 on v0

v2 whole, which is shorter than its diff:
```python
import functools

import jax
import jax.numpy as jnp
from jax import lax
from jax.experimental import pallas as pl
from jax.experimental.pallas import tpu as pltpu
from jax.sharding import PartitionSpec as P

ROWS = 8
SLOTS = 6
LEAD = 8
SOME = 4
TAIL = 4
PEERS = pl.DeviceIdType.MESH


def spans(batch, ends):
    ends = tuple(range(SOME, batch - TAIL + 1, SOME)) + tuple(batch - TAIL + e for e in ends)
    return tuple(zip((0,) + ends[:-1], ends))


def kernel(n, q_hbm, k_hbm, v_hbm, o_ref, qbuf, kbuf, vbuf, wbuf, parts, stats, share, *sems):
    q_sem, k_sem, v_sem, tail_sem, go_sem, came_sem, out_sem, in_sem = sems
    batch, heads, dim = q_hbm.shape
    chunks, wide = heads // ROWS, ROWS * dim
    last = batch - 1
    me = lax.axis_index("sp")
    f32 = jnp.float32
    runs, segments = spans(batch, (2, 4)), spans(batch, (2, 3, 4))
    many = (batch - TAIL) // SOME

    def fetch(hbm, buf, sem, b):
        slot = lax.rem(b, SLOTS)
        return pltpu.make_async_copy(hbm.at[b], buf.at[slot], sem.at[slot])

    def piece(c):
        rows = pl.ds(c * wide, wide)
        return pltpu.make_async_copy(v_hbm.at[last, rows], vbuf.at[last % SLOTS, rows], tail_sem.at[c])

    def more(t):
        @pl.when(t + SLOTS < batch)
        def _():
            fetch(k_hbm, kbuf, k_sem, t + SLOTS).start(priority=1)

        @pl.when(jnp.logical_and(t - LEAD + SLOTS >= 0, t - LEAD + SLOTS < last))
        def _():
            fetch(v_hbm, vbuf, v_sem, t - LEAD + SLOTS).start(priority=1)

        @pl.when(t - LEAD + SLOTS == last)
        def _():
            for c in range(chunks):
                piece(c).start(priority=1)

    q_copy = pltpu.make_async_copy(q_hbm, qbuf, q_sem)
    q_copy.start()
    for b in range(SLOTS):
        fetch(k_hbm, kbuf, k_sem, b).start(priority=1)
        if b >= LEAD:
            fetch(v_hbm, vbuf, v_sem, b - LEAD).start(priority=1)

    barrier = pltpu.get_barrier_semaphore()
    for j in range(1, n):
        pl.semaphore_signal(barrier, inc=1, device_id={"sp": lax.rem(me + j, n)}, device_id_type=PEERS)

    row = lax.broadcasted_iota(jnp.int32, (ROWS, wide), 0)
    block = lax.broadcasted_iota(jnp.int32, (ROWS, wide), 1) // dim
    own = [block == row, block == row + 1 - 2 * (row % 2)]
    head = lax.broadcasted_iota(jnp.int32, (ROWS, 128), 0)
    lane = lax.broadcasted_iota(jnp.int32, (ROWS, 128), 1)
    even = (head % 2) == 0

    def run_of(b):
        return jnp.where(b < batch - TAIL, lax.div(b, SOME), many + lax.div(b - (batch - TAIL), 2))

    def place(b, c):
        return lax.rem(b, SOME) * chunks + c

    def swap(x):
        odd = lax.broadcasted_iota(jnp.int32, x.shape, 0) % 2
        return jnp.where(odd == 0, pltpu.roll(x, ROWS - 1, 0), pltpu.roll(x, 1, 0))

    def score(b):
        slot, g = lax.rem(b, SLOTS), run_of(b)
        line = jnp.where(lax.rem(b, SOME) == 0, 0.0, stats[me, g])
        for c in range(chunks):
            query = qbuf[b, c * ROWS : (c + 1) * ROWS, :].astype(f32)
            if c % 2:
                query = swap(query)
            spread = jnp.where(own[c % 2], jnp.concatenate([query] * ROWS, axis=1), 0.0).astype(jnp.bfloat16)
            s = jnp.dot(spread, kbuf[slot, c * wide : (c + 1) * wide, :], preferred_element_type=f32) * dim**-0.5
            high = jnp.max(s, -1, keepdims=True)
            w = jnp.exp(s - high)
            wbuf[lax.rem(b, LEAD + 1), c] = w.astype(jnp.bfloat16)
            line = jnp.where(lane == place(b, c), high, line)
            line = jnp.where(lane == 64 + place(b, c), jnp.sum(w, -1, keepdims=True), line)
        stats[me, g] = line

    def weights(b):
        return [wbuf[lax.rem(b, LEAD + 1), c] for c in range(chunks)]

    def see(b, weight, ready=lambda c: None):
        slot = lax.rem(b, SLOTS)
        shares = share[...]
        seen = []
        for c in range(chunks):
            ready(c)
            mine = jnp.sum(jnp.where(lane == place(b, c), shares, 0.0), -1, keepdims=True)
            r = lax.dot_general(weight[c], vbuf[slot, c * wide : (c + 1) * wide, :], (((1,), (1,)), ((), ())), preferred_element_type=f32)
            r = jnp.where(own[c % 2], r, 0.0)
            seen.append(sum(r[:, i * 128 : (i + 1) * 128] for i in range(wide // 128)) * mine)
        pairs = [seen[c] + seen[c + 1] for c in range(0, chunks, 2)]
        parts[me, b] = jnp.concatenate(pairs, 0).astype(jnp.bfloat16)

    def remote(ref, out, came, to):
        return pltpu.make_async_remote_copy(src_ref=ref, dst_ref=ref, send_sem=out, recv_sem=came, device_id={"sp": to}, device_id_type=PEERS)

    def ahead(j):
        return lax.rem(me + j, n)

    def behind(j):
        return lax.rem(me + n - j, n)

    def line_to(g, j, source):
        return remote(stats.at[source, g], go_sem.at[g, j - 1], came_sem.at[g, j - 1], ahead(j))

    def part_to(s, lo, size, j, source):
        return remote(parts.at[source, pl.ds(lo, size)], out_sem.at[s, j - 1], in_sem.at[s, j - 1], ahead(j))

    def send_lines(g):
        for j in range(1, n):
            line_to(g, j, me).start()

    def send_parts(s, lo, size):
        for j in range(1, n):
            part_to(s, lo, size, j, me).start()

    def weigh(g):
        for j in range(1, n):
            line_to(g, j, behind(j)).wait_recv()
        high = functools.reduce(jnp.maximum, [stats[i, g] for i in range(n)])
        total = sum(pltpu.roll(stats[i, g], 64, 1) * jnp.exp(stats[i, g] - high) for i in range(n))
        share[...] = jnp.exp(stats[me, g] - high) / total

    def scored(t):
        whole = jnp.logical_and(lax.rem(t, SOME) == SOME - 1, t < batch - TAIL)
        pl.when(whole)(lambda: send_lines(lax.div(t, SOME)))
        for g, (lo, hi) in list(enumerate(runs))[many:]:
            pl.when(t == hi - 1)(functools.partial(send_lines, g))

    def first_of(b):
        whole = jnp.logical_and(lax.rem(b, SOME) == 0, b < batch - TAIL)
        pl.when(whole)(lambda: weigh(lax.div(b, SOME)))

    def seen_all(b):
        whole = jnp.logical_and(lax.rem(b, SOME) == SOME - 1, b < batch - TAIL)
        pl.when(whole)(lambda: send_parts(lax.div(b, SOME), b - (SOME - 1), SOME))

    def body(t, nothing):
        f = t - LEAD
        first_of(f)
        fetch(k_hbm, kbuf, k_sem, t).wait()
        fetch(v_hbm, vbuf, v_sem, f).wait()
        held = weights(f)
        score(t)
        see(f, held)
        more(t)
        scored(t)
        seen_all(f)
        return nothing

    q_copy.wait()
    for t in range(LEAD):
        fetch(k_hbm, kbuf, k_sem, t).wait()
        score(jnp.int32(t))
        more(jnp.int32(t))
        if t == SOME - 1:
            pl.semaphore_wait(barrier, n - 1)
        if t % SOME == SOME - 1:
            send_lines(t // SOME)
    lax.fori_loop(LEAD, batch, body, 0)
    b = batch - LEAD
    while b < batch:
        size = 2 if b + 2 < last else 1
        for x in range(b, b + size):
            for g, (lo, hi) in enumerate(runs):
                if lo == x:
                    weigh(g)
            if x < last:
                fetch(v_hbm, vbuf, v_sem, x).wait()
        for x in range(b, b + size):
            see(x, weights(x), (lambda c: piece(c).wait()) if x == last else (lambda c: None))
        for x in range(b, b + size):
            more(jnp.int32(x + LEAD))
        for x in range(b, b + size):
            for s, (lo, hi) in enumerate(segments):
                if hi - 1 == x:
                    send_parts(s, lo, hi - lo)
        b += size

    for s, (lo, hi) in enumerate(segments):
        for j in range(1, n):
            part_to(s, lo, hi - lo, j, behind(j)).wait_recv()
        for b in range(lo, hi):
            x = sum(parts[i, b].astype(f32) for i in range(n))
            out = []
            for p in range(chunks // 2):
                y = x[p * ROWS : (p + 1) * ROWS]
                z = pltpu.roll(y, dim, 1)
                out += [jnp.where(even, y, z)[:, :dim], swap(jnp.where(even, z, y))[:, :dim]]
            o_ref[b] = jnp.concatenate(out, 0).astype(o_ref.dtype)
    for j in range(1, n):
        for g in range(len(runs)):
            line_to(g, j, me).wait_send()
        for s, (lo, hi) in enumerate(segments):
            part_to(s, lo, hi - lo, j, me).wait_send()


def solution(mesh):
    n = mesh.shape["sp"]

    def step(q, k, v):
        batch, tokens, heads, dim = k.shape
        k, v = (x.transpose(0, 2, 3, 1).reshape(batch, heads * dim, tokens) for x in (k, v))
        chunks = heads // ROWS
        runs, segments = len(spans(batch, (2, 4))), len(spans(batch, (2, 3, 4)))
        hbm = pl.BlockSpec(memory_space=pl.ANY)
        dma = pltpu.SemaphoreType.DMA
        return pl.pallas_call(
            functools.partial(kernel, n),
            out_shape=jax.ShapeDtypeStruct(q.shape, q.dtype),
            in_specs=[hbm] * 3,
            out_specs=pl.BlockSpec(memory_space=pltpu.VMEM),
            scratch_shapes=[
                pltpu.VMEM(q.shape, q.dtype),
                pltpu.VMEM((SLOTS, heads * dim, tokens), k.dtype),
                pltpu.VMEM((SLOTS, heads * dim, tokens), v.dtype),
                pltpu.VMEM((LEAD + 1, chunks, ROWS, tokens), jnp.bfloat16),
                pltpu.VMEM((n, batch, heads // 2, 2 * dim), jnp.bfloat16),
                pltpu.VMEM((n, runs, ROWS, 128), jnp.float32),
                pltpu.VMEM((ROWS, 128), jnp.float32),
                dma,
                dma((SLOTS,)),
                dma((SLOTS,)),
                dma((chunks,)),
                dma((runs, n - 1)),
                dma((runs, n - 1)),
                dma((segments, n - 1)),
                dma((segments, n - 1)),
            ],
            compiler_params=pltpu.CompilerParams(collective_id=0, has_side_effects=True, vmem_limit_bytes=56114023),
            cost_estimate=pl.CostEstimate(flops=4 * k.size, bytes_accessed=4 * k.size, transcendentals=batch * heads * tokens),
        )(q, k, v)

    return jax.shard_map(
        step,
        mesh=mesh,
        in_specs=(P("dp", None, None), P("dp", "sp", None, None), P("dp", "sp", None, None)),
        out_specs=P("dp", None, None),
        check_vma=False,
    )
```

time: 112 us -> 51.3 us (0.46)
  Pallas kernels: 0 us -> 50.5 us
  matrix products: 48.3 us -> 0 us
  waiting for transfers between devices: 31.3 us -> 0 us
  between operations: 13.5 us -> 0.01 us
  local copies, waits for them, and re-layouts: 9.44 us -> 0.71 us
  other arithmetic: 8.72 us -> 0 us
    pallas_call x0 -> x1, Pallas kernels: none -> 50.5 us  [step(): pl.pallas_call(functools.partial(kernel, n), out_shape=jax.ShapeDtypeStru...]
    dot_general x2 -> x0, matrix products: 48.3 us -> none  [einsum(): return jnp.einsum(form, a.astype(jnp.float32), b.astype(jnp.float32))]
    all_gather x1 -> x0, waiting for transfers between devices: 31.2 us -> none  [step(): return together(lax.all_gather(part_of(q, k, v), 'sp')).reshape(q.shape)]
    all_gather x1 -> x0, local copies, waits for them, and re-layouts: 7.62 us -> none  [step(): return together(lax.all_gather(part_of(q, k, v), 'sp')).reshape(q.shape)]
    reduce_sum x2 -> x0, other arithmetic: 5.69 us -> none  [the longest x1 4.69 us: together(): jnp.sum(seen * scale, 0) / jnp.sum(total * scale, 0)]
    convert_element_type x1 -> x0, local copies, waits for them, and re-layouts: 1.27 us -> none  [together(): (jnp.sum(seen * scale, 0) / jnp.sum(total * scale, 0)).astype(jnp.bfloat16)]
    concatenate x1 -> x0, other arithmetic: 1.18 us -> none  [part_of(): jnp.concatenate([seen, jnp.sum(weights, -1, keepdims=True), high], -1)]
    reduce_max x2 -> x0, other arithmetic: 1.15 us -> none  [the longest x1 0.92 us: together(): scale = jnp.exp(high - jnp.max(high, 0))]
  transfers between devices with their start and end apart: 1 -> 0, of which waited for: 1 -> 0; matrix products, arithmetic and copies ran while one was open for 0% -> 0% of each run, Pallas kernels for 0% -> 0%
where the time goes in v2:
time: 51.3 us; the launch traced here: 51.2 us
  Pallas kernels  50.5 us (98%)
  local copies, waits for them, and re-layouts  0.71 us (1%)
    pallas_call x1, Pallas kernels, step(): pl.pallas_call(functools.partial(kernel, n), out_shape=jax.ShapeDtypeStru...  50.5 us

profile of v2, /device:TPU:113, one launch (start us, length us, event | category | flops | bytes accessed | tf_op | source)
XLA Modules:
  0.0 51.2 jit_solution(10854945992918298363)
XLA Ops:
  0.0 50.5 %shard_map.37 = bf16[32,32,64]{2,1,0:T(8,128)(2,1)S(1)} custom-call(bf16[32,32,64]{2,1,0:T(8,128)(2,1)} %q_hbm.1, bf16[32,2048,512]{2,1,0:T(8,128)(2,1)} %bitcast.1.k_hbm, bf16[32,2048,512]{2,1,0:T(8,128)(2,1)} %bitcast.3.v_hbm), custom_call_target="tpu_custom_call" | custom-call | flops 134217728 | bytes 134217728 | tf_op jit(solution)/shard_map/pallas_call | solution.py:229
  50.5 0.7 %copy.5 = bf16[32,32,64]{2,1,0:T(8,128)(2,1)} copy(bf16[32,32,64]{2,1,0:T(8,128)(2,1)S(1)} %shard_map.37) | data formatting | bytes 262144

commit v3 on v2

--- a/solution.py
+++ b/solution.py
@@ -12,6 +12,7 @@
 LEAD = 8
 SOME = 4
 TAIL = 4
+STEPS = (2, 2, 2, 1, 1)
 PEERS = pl.DeviceIdType.MESH
 
 
@@ -21,36 +22,28 @@
 
 
 def kernel(n, q_hbm, k_hbm, v_hbm, o_ref, qbuf, kbuf, vbuf, wbuf, parts, stats, share, *sems):
-    q_sem, k_sem, v_sem, tail_sem, go_sem, came_sem, out_sem, in_sem = sems
+    q_sem, k_sem, v_sem, go_sem, came_sem, out_sem, in_sem = sems
     batch, heads, dim = q_hbm.shape
     chunks, wide = heads // ROWS, ROWS * dim
     last = batch - 1
     me = lax.axis_index("sp")
     f32 = jnp.float32
     runs, segments = spans(batch, (2, 4)), spans(batch, (2, 3, 4))
+    order = sorted(range(1, n), key=lambda j: abs(j - n // 2))
     many = (batch - TAIL) // SOME
 
     def fetch(hbm, buf, sem, b):
         slot = lax.rem(b, SLOTS)
         return pltpu.make_async_copy(hbm.at[b], buf.at[slot], sem.at[slot])
-
-    def piece(c):
-        rows = pl.ds(c * wide, wide)
-        return pltpu.make_async_copy(v_hbm.at[last, rows], vbuf.at[last % SLOTS, rows], tail_sem.at[c])
 
     def more(t):
         @pl.when(t + SLOTS < batch)
         def _():
             fetch(k_hbm, kbuf, k_sem, t + SLOTS).start(priority=1)
 
-        @pl.when(jnp.logical_and(t - LEAD + SLOTS >= 0, t - LEAD + SLOTS < last))
+        @pl.when(jnp.logical_and(t - LEAD + SLOTS >= 0, t - LEAD + SLOTS < batch))
         def _():
             fetch(v_hbm, vbuf, v_sem, t - LEAD + SLOTS).start(priority=1)
-
-        @pl.when(t - LEAD + SLOTS == last)
-        def _():
-            for c in range(chunks):
-                piece(c).start(priority=1)
 
     q_copy = pltpu.make_async_copy(q_hbm, qbuf, q_sem)
     q_copy.start()
@@ -99,12 +92,11 @@
     def weights(b):
         return [wbuf[lax.rem(b, LEAD + 1), c] for c in range(chunks)]
 
-    def see(b, weight, ready=lambda c: None):
+    def see(b, weight):
         slot = lax.rem(b, SLOTS)
         shares = share[...]
         seen = []
         for c in range(chunks):
-            ready(c)
             mine = jnp.sum(jnp.where(lane == place(b, c), shares, 0.0), -1, keepdims=True)
             r = lax.dot_general(weight[c], vbuf[slot, c * wide : (c + 1) * wide, :], (((1,), (1,)), ((), ())), preferred_element_type=f32)
             r = jnp.where(own[c % 2], r, 0.0)
@@ -118,26 +110,25 @@
     def ahead(j):
         return lax.rem(me + j, n)
 
-    def behind(j):
-        return lax.rem(me + n - j, n)
-
-    def line_to(g, j, source):
-        return remote(stats.at[source, g], go_sem.at[g, j - 1], came_sem.at[g, j - 1], ahead(j))
-
-    def part_to(s, lo, size, j, source):
-        return remote(parts.at[source, pl.ds(lo, size)], out_sem.at[s, j - 1], in_sem.at[s, j - 1], ahead(j))
+    def line_to(g, j):
+        return remote(stats.at[me, g], go_sem, came_sem.at[g], ahead(j))
+
+    def part_to(x, lo, size, j):
+        return remote(parts.at[me, pl.ds(lo, size)], out_sem, in_sem.at[x], ahead(j))
+
+    def all_but_one(ref, out, came):
+        return remote(ref, out, came, ahead(1))
 
     def send_lines(g):
-        for j in range(1, n):
-            line_to(g, j, me).start()
-
-    def send_parts(s, lo, size):
-        for j in range(1, n):
-            part_to(s, lo, size, j, me).start()
+        for j in order:
+            line_to(g, j).start()
+
+    def send_parts(x, lo, size):
+        for j in order:
+            part_to(x, lo, size, j).start()
 
     def weigh(g):
-        for j in range(1, n):
-            line_to(g, j, behind(j)).wait_recv()
+        all_but_one(stats.at[pl.ds(0, n - 1), g], go_sem, came_sem.at[g]).wait_recv()
         high = functools.reduce(jnp.maximum, [stats[i, g] for i in range(n)])
         total = sum(pltpu.roll(stats[i, g], 64, 1) * jnp.exp(stats[i, g] - high) for i in range(n))
         share[...] = jnp.exp(stats[me, g] - high) / total
@@ -154,7 +145,7 @@
 
     def seen_all(b):
         whole = jnp.logical_and(lax.rem(b, SOME) == SOME - 1, b < batch - TAIL)
-        pl.when(whole)(lambda: send_parts(lax.div(b, SOME), b - (SOME - 1), SOME))
+        pl.when(whole)(lambda: send_parts(0, b - (SOME - 1), SOME))
 
     def body(t, nothing):
         f = t - LEAD
@@ -180,27 +171,26 @@
             send_lines(t // SOME)
     lax.fori_loop(LEAD, batch, body, 0)
     b = batch - LEAD
-    while b < batch:
-        size = 2 if b + 2 < last else 1
+    for size in STEPS:
         for x in range(b, b + size):
             for g, (lo, hi) in enumerate(runs):
                 if lo == x:
                     weigh(g)
-            if x < last:
-                fetch(v_hbm, vbuf, v_sem, x).wait()
-        for x in range(b, b + size):
-            see(x, weights(x), (lambda c: piece(c).wait()) if x == last else (lambda c: None))
+            fetch(v_hbm, vbuf, v_sem, x).wait()
+        for x in range(b, b + size):
+            see(x, weights(x))
         for x in range(b, b + size):
             more(jnp.int32(x + LEAD))
         for x in range(b, b + size):
-            for s, (lo, hi) in enumerate(segments):
+            for lo, hi in segments:
                 if hi - 1 == x:
-                    send_parts(s, lo, hi - lo)
+                    send_parts(max(0, segments.index((lo, hi)) - many + 1), lo, hi - lo)
         b += size
 
-    for s, (lo, hi) in enumerate(segments):
-        for j in range(1, n):
-            part_to(s, lo, hi - lo, j, behind(j)).wait_recv()
+    for x, (lo, hi) in enumerate(((0, batch - TAIL),) + segments[many:]):
+        if hi == batch:
+            all_but_one(stats.at[pl.ds(0, n - 1)], go_sem, came_sem.at[0]).wait_send()
+        all_but_one(parts.at[pl.ds(0, n - 1), pl.ds(lo, hi - lo)], out_sem, in_sem.at[x]).wait_recv()
         for b in range(lo, hi):
             x = sum(parts[i, b].astype(f32) for i in range(n))
             out = []
@@ -209,11 +199,7 @@
                 z = pltpu.roll(y, dim, 1)
                 out += [jnp.where(even, y, z)[:, :dim], swap(jnp.where(even, z, y))[:, :dim]]
             o_ref[b] = jnp.concatenate(out, 0).astype(o_ref.dtype)
-    for j in range(1, n):
-        for g in range(len(runs)):
-            line_to(g, j, me).wait_send()
-        for s, (lo, hi) in enumerate(segments):
-            part_to(s, lo, hi - lo, j, me).wait_send()
+    all_but_one(parts.at[pl.ds(0, n - 1)], out_sem, in_sem.at[0]).wait_send()
 
 
 def solution(mesh):
@@ -242,11 +228,10 @@
                 dma,
                 dma((SLOTS,)),
                 dma((SLOTS,)),
-                dma((chunks,)),
-                dma((runs, n - 1)),
-                dma((runs, n - 1)),
-                dma((segments, n - 1)),
-                dma((segments, n - 1)),
+                dma,
+                dma((runs,)),
+                dma,
+                dma((segments - (batch - TAIL) // SOME + 1,)),
             ],
             compiler_params=pltpu.CompilerParams(collective_id=0, has_side_effects=True, vmem_limit_bytes=56114023),
             cost_estimate=pl.CostEstimate(flops=4 * k.size, bytes_accessed=4 * k.size, transcendentals=batch * heads * tokens),

time: 51.3 us -> 48.4 us (0.943)
  Pallas kernels: 50.5 us -> 47.6 us
    pallas_call x1, Pallas kernels: 50.5 us -> 47.6 us  [step(): pl.pallas_call(functools.partial(kernel, n), out_shape=jax.ShapeDtypeStru...]
where the time goes in v3:
time: 48.4 us; the launch traced here: 48.3 us
  Pallas kernels  47.6 us (98%)
  local copies, waits for them, and re-layouts  0.71 us (1%)
    pallas_call x1, Pallas kernels, step(): pl.pallas_call(functools.partial(kernel, n), out_shape=jax.ShapeDtypeStru...  47.6 us

profile of v3, /device:TPU:113, one launch (start us, length us, event | category | flops | bytes accessed | tf_op | source)
XLA Modules:
  0.0 48.3 jit_solution(14198631629922298319)
XLA Ops:
  0.0 47.6 %shard_map.37 = bf16[32,32,64]{2,1,0:T(8,128)(2,1)S(1)} custom-call(bf16[32,32,64]{2,1,0:T(8,128)(2,1)} %q_hbm.1, bf16[32,2048,512]{2,1,0:T(8,128)(2,1)} %bitcast.1.k_hbm, bf16[32,2048,512]{2,1,0:T(8,128)(2,1)} %bitcast.3.v_hbm), custom_call_target="tpu_custom_call" | custom-call | flops 134217728 | bytes 134217728 | tf_op jit(solution)/shard_map/pallas_call | solution.py:215
  47.6 0.7 %copy.5 = bf16[32,32,64]{2,1,0:T(8,128)(2,1)} copy(bf16[32,32,64]{2,1,0:T(8,128)(2,1)S(1)} %shard_map.37) | data formatting | bytes 262144

commit v4 on v3

--- a/solution.py
+++ b/solution.py
@@ -127,8 +127,10 @@
         for j in order:
             part_to(x, lo, size, j).start()
 
+    def lines_in(g):
+        all_but_one(stats.at[pl.ds(0, n - 1), g], go_sem, came_sem.at[g]).wait_recv()
+
     def weigh(g):
-        all_but_one(stats.at[pl.ds(0, n - 1), g], go_sem, came_sem.at[g]).wait_recv()
         high = functools.reduce(jnp.maximum, [stats[i, g] for i in range(n)])
         total = sum(pltpu.roll(stats[i, g], 64, 1) * jnp.exp(stats[i, g] - high) for i in range(n))
         share[...] = jnp.exp(stats[me, g] - high) / total
@@ -141,7 +143,12 @@
 
     def first_of(b):
         whole = jnp.logical_and(lax.rem(b, SOME) == 0, b < batch - TAIL)
-        pl.when(whole)(lambda: weigh(lax.div(b, SOME)))
+
+        @pl.when(whole)
+        def _():
+            lines_in(lax.div(b, SOME))
+            weigh(lax.div(b, SOME))
+
 
     def seen_all(b):
         whole = jnp.logical_and(lax.rem(b, SOME) == SOME - 1, b < batch - TAIL)
@@ -171,21 +178,25 @@
             send_lines(t // SOME)
     lax.fori_loop(LEAD, batch, body, 0)
     b = batch - LEAD
+    due = []
     for size in STEPS:
+        new = [g for g, (lo, hi) in enumerate(runs) if lo == b]
+        for g in new:
+            lines_in(g)
         for x in range(b, b + size):
-            for g, (lo, hi) in enumerate(runs):
-                if lo == x:
-                    weigh(g)
             fetch(v_hbm, vbuf, v_sem, x).wait()
+        for one in due:
+            send_parts(*one)
+        for g in new:
+            weigh(g)
         for x in range(b, b + size):
             see(x, weights(x))
         for x in range(b, b + size):
             more(jnp.int32(x + LEAD))
-        for x in range(b, b + size):
-            for lo, hi in segments:
-                if hi - 1 == x:
-                    send_parts(max(0, segments.index((lo, hi)) - many + 1), lo, hi - lo)
         b += size
+        due = [(max(0, i - many + 1), lo, hi - lo) for i, (lo, hi) in enumerate(segments) if b - size < hi <= b]
+    for one in due:
+        send_parts(*one)
 
     for x, (lo, hi) in enumerate(((0, batch - TAIL),) + segments[many:]):
         if hi == batch:

time: 48.4 us -> 48.3 us (level)
  no operation moved by 1% of the time
where the time goes in v4:
time: 48.3 us; the launch traced here: 48.2 us
  Pallas kernels  47.5 us (98%)
  local copies, waits for them, and re-layouts  0.71 us (1%)
    pallas_call x1, Pallas kernels, step(): pl.pallas_call(functools.partial(kernel, n), out_shape=jax.ShapeDtypeStru...  47.5 us

profile of v4, /device:TPU:113, one launch (start us, length us, event | category | flops | bytes accessed | tf_op | source)
XLA Modules:
  0.0 48.2 jit_solution(4465163779382625355)
XLA Ops:
  0.0 47.5 %shard_map.37 = bf16[32,32,64]{2,1,0:T(8,128)(2,1)S(1)} custom-call(bf16[32,32,64]{2,1,0:T(8,128)(2,1)} %q_hbm.1, bf16[32,2048,512]{2,1,0:T(8,128)(2,1)} %bitcast.1.k_hbm, bf16[32,2048,512]{2,1,0:T(8,128)(2,1)} %bitcast.3.v_hbm), custom_call_target="tpu_custom_call" | custom-call | flops 134217728 | bytes 134217728 | tf_op jit(solution)/shard_map/pallas_call | solution.py:226
  47.5 0.7 %copy.5 = bf16[32,32,64]{2,1,0:T(8,128)(2,1)} copy(bf16[32,32,64]{2,1,0:T(8,128)(2,1)S(1)} %shard_map.37) | data formatting | bytes 262144
